TPU v7x, 32 devices: a whole 2x2x4 slice. The times are simulated.
32 devices in a mesh: tm: 4 (over y, x), space: 8 (over z, core).
Axes of the slice: x: 2, y: 2, z: 4, core: 2. Of those that a mesh axis runs over, the one named last changes fastest.
Arguments:
- thermal_field: float32 [128, 49152], P(('tm', 'space')), may hold values from 245 to 255
- seasonal_bucket: int32 [128], replicated, may hold values from 0 to 45, as said below
- season_of_record: int32 [128], replicated, may hold values from 0 to 7
Outputs:
- anomaly: float32 [128, 49152], P(('tm', 'space'))
Inputs may be any that keep to these rules, and one draw needn't show every extreme that they name: `seasonal_bucket`: every group holds at least one day whose year is below 6.
All inputs are finite; a program needn't handle non-finite values.
Results may differ from a plain program's by a relative error of at most 0.0003.
Values sent between devices are 32-bit elements; how exact they have to be, the bound alone decides.
A program may use at most 64 MiB of HBM per device.

v0:
```python
import functools

import jax
import jax.numpy as jnp
from jax import lax
from jax.experimental import pallas as pl
from jax.experimental.pallas import tpu as pltpu
from jax.sharding import PartitionSpec as P

GROUPS = 46
BASE_YEARS = 6
CHUNKS = 8
LAG = 2
LEAD = 3
SHARE = 2
MESH = pl.DeviceIdType.MESH


def exact_dot(mask, x):
    high = x.astype(jnp.bfloat16)
    rest = x - high.astype(jnp.float32)
    middle = rest.astype(jnp.bfloat16)
    low = (rest - middle.astype(jnp.float32)).astype(jnp.bfloat16)
    total = jnp.dot(mask, low, preferred_element_type=jnp.float32)
    total += jnp.dot(mask, middle, preferred_element_type=jnp.float32)
    return total + jnp.dot(mask, high, preferred_element_type=jnp.float32)


def kernel(nt, ns, chunks, lag, lead, x_hbm, bucket_hbm, season_hbm, out_ref,
           calendar, date_sem, xv, recv, sums, other, y, load_sem,
           send1, recv1, send2, recv2, send3, recv3,
           got, done, send4, recv4, send5, recv5):
    nh, nq = ns // 2, ns // 4
    half, owners = nt * nh, nt * nq
    when = chunks - 1
    when_other = chunks // 2
    rows, cells = x_hbm.shape
    n = nt * ns
    direct = cells // SHARE // n
    start = direct * n
    mine = (cells - start) // owners
    c = mine // chunks
    days = rows * nt * ns
    t, s = lax.axis_index("tm"), lax.axis_index("space")
    h = s // nh
    local = s - h * nh
    first = nq * (1 - h)
    place = local - first
    is_owner = (place >= 0) & (place < nq)
    slot = t * nh + local
    partner = s + nq * (1 - 2 * h)

    load = pltpu.make_async_copy(x_hbm, xv, load_sem)
    load.start()
    dates = [pltpu.make_async_copy(ref, calendar.at[i], date_sem.at[i])
             for i, ref in enumerate((bucket_hbm, season_hbm))]
    for date in dates:
        date.start()

    def to_owners(body, others):
        for dq in range(nq):
            for dt in range(nt):
                if others and dt == dq == 0:
                    continue
                pt, pq = lax.rem(t + dt, nt), lax.rem(place + nq + dq, nq)
                body(pt, h * nh + first + pq, pt * nq + pq)

    def to_half(body):
        for dl in [(nh // 2 + i) % nh for i in range(nh)]:
            for dt in range(nt):
                if dt == dl == 0:
                    continue
                pt, at = lax.rem(t + dt, nt), lax.rem(local + dl, nh)
                body(pt, h * nh + at, pt * nh + at)

    barrier = pltpu.get_barrier_semaphore()

    def greet(pt, ps, p):
        pl.semaphore_signal(barrier, inc=1, device_id=(pt, ps), device_id_type=MESH)

    def to_all(body):
        for ds in [(nh + i) % ns for i in range(ns)]:
            for dt in range(nt):
                if dt == ds == 0:
                    continue
                pt, ps = lax.rem(t + dt, nt), lax.rem(s + ds, ns)
                body(pt, ps, pt * ns + ps)

    to_all(greet)
    pl.semaphore_wait(barrier, n - 1)
    who = t * ns + s
    own = pl.ds(pl.multiple_of(who * direct, 128), direct)

    def push(k, others):
        def one(pt, ps, p):
            pltpu.make_async_remote_copy(
                src_ref=xv.at[:, pl.ds(pl.multiple_of(start + p * mine + k * c, 128), c)],
                dst_ref=recv.at[k, slot], send_sem=send1.at[k], recv_sem=recv1.at[k],
                device_id=(pt, ps), device_id_type=MESH).start()
        to_owners(one, others)

    load.wait()

    def push_direct(pt, ps, p):
        pltpu.make_async_remote_copy(
            src_ref=xv.at[:, pl.ds(pl.multiple_of(p * direct, 128), direct)],
            dst_ref=got.at[who], send_sem=send4, recv_sem=recv4,
            device_id=(pt, ps), device_id_type=MESH).start()
    to_all(push_direct)
    got[who] = xv[:, own]
    for date in dates:
        date.wait()

    def all_direct(sem):
        part = got.at[pl.ds(0, n - 1)]
        pltpu.make_async_copy(part, part, sem).wait()

    def finish_direct():
        bucket = jnp.broadcast_to(calendar[0], (days, days))
        season = jnp.broadcast_to(calendar[1], (days, days))
        same = jnp.where((bucket == bucket.T) & (season < BASE_YEARS), 1.0, 0.0)
        inverse = 1.0 / jnp.sum(same, axis=1, keepdims=True)
        all_direct(recv4)
        x = got[...].reshape(days, direct)
        mean = exact_dot(same.astype(jnp.bfloat16), x) * inverse
        done[...] = (x - mean).reshape(n, rows, direct)

        def back_direct(pt, ps, p):
            pltpu.make_async_remote_copy(
                src_ref=done.at[p], dst_ref=out_ref.at[:, own],
                send_sem=send5, recv_sem=recv5,
                device_id=(pt, ps), device_id_type=MESH).start()
        to_all(back_direct)
        out_ref[:, own] = done[who]

    def all_of(count, sem):
        part = recv.at[0, pl.ds(0, count)]
        pltpu.make_async_copy(part, part, sem).wait()

    @pl.when(is_owner)
    def _():
        for k in range(min(lead, chunks)):
            push(k, True)
        me = t * nq + place
        base = pl.multiple_of(start + me * mine, 128)
        padded = sums.shape[1]

        bucket, season = calendar[0], calendar[1]
        key = jnp.where(season < BASE_YEARS, bucket, -1)
        width = nh * rows
        here = half * rows
        order = lax.broadcasted_iota(jnp.int32, (here, days), 0)
        day = (order // width) * (2 * width) + h * width + lax.rem(order, width)
        pick = day == lax.broadcasted_iota(jnp.int32, (here, days), 1)

        def of_half(row):
            return jnp.sum(jnp.where(pick, row, 0), axis=1, keepdims=True)

        member = of_half(bucket) == lax.broadcasted_iota(jnp.int32, (here, padded), 1)
        member = jnp.where(member, 1.0, 0.0).astype(jnp.bfloat16)
        key_row = jnp.broadcast_to(of_half(key), (here, here)).T[:1]
        group = lax.broadcasted_iota(jnp.int32, (padded, here), 0)
        baseline = jnp.where(group == key_row, 1.0, 0.0).astype(jnp.bfloat16)
        counted = lax.broadcasted_iota(jnp.int32, (padded, days), 0) == key
        counts = jnp.sum(jnp.where(counted, 1.0, 0.0), axis=1, keepdims=True)
        inverse = 1.0 / jnp.maximum(counts, 1.0)

        def swap(k):
            return pltpu.make_async_remote_copy(
                src_ref=sums.at[k], dst_ref=other.at[k],
                send_sem=send2.at[k], recv_sem=recv2.at[k],
                device_id=(t, partner), device_id_type=MESH)

        def finish(k):
            swap(k).wait_recv()
            climate = (sums[k] + other[k]) * inverse
            x = recv[k].reshape(here, c)
            y[k] = (x - exact_dot(member, climate)).reshape(half, rows, c)
            at = pl.ds(pl.multiple_of(base + k * c, 128), c)

            def back(pt, ps, p):
                pltpu.make_async_remote_copy(
                    src_ref=y.at[k, p], dst_ref=out_ref.at[:, at],
                    send_sem=send3.at[k], recv_sem=recv3.at[k],
                    device_id=(pt, ps), device_id_type=MESH).start()
            to_half(back)
            out_ref[:, at] = y[k, slot]

        for k in range(chunks):
            if k + lead < chunks:
                push(k + lead, True)
            recv[k, slot] = xv[:, pl.ds(pl.multiple_of(base + k * c, 128), c)]
            all_of(half - 1, recv1.at[k])
            sums[k] = exact_dot(baseline, recv[k].reshape(here, c))
            swap(k).start()
            if k == when:
                finish_direct()
            if k >= lag:
                finish(k - lag)
        for k in range(max(chunks - lag, 0), chunks):
            finish(k)

        for k in range(chunks):
            all_of(owners - 1, send1.at[k])
            swap(k).wait_send()
            all_of(owners - 1, recv3.at[k])
            all_of(half - 1, send3.at[k])

    @pl.when(jnp.logical_not(is_owner))
    def _():
        for k in range(chunks):
            push(k, False)
        for k in range(chunks):
            all_of(owners, send1.at[k])
            if k == when_other:
                finish_direct()
            all_of(owners, recv3.at[k])

    all_direct(send4)
    all_direct(recv5)
    all_direct(send5)


def solution(mesh):
    nt, ns = mesh.shape["tm"], mesh.shape["space"]
    half, owners = nt * (ns // 2), nt * (ns // 4)

    def shards(thermal_field, seasonal_bucket, season_of_record):
        rows, cells = thermal_field.shape
        n = nt * ns
        direct = cells // SHARE // n
        c, days = (cells - direct * n) // owners // CHUNKS, rows * n
        sems = pltpu.SemaphoreType.DMA
        per_chunk = sems((CHUNKS,))
        vmem = functools.partial(pltpu.VMEM, dtype=jnp.float32)
        return pl.pallas_call(
            functools.partial(kernel, nt, ns, CHUNKS, LAG, LEAD),
            out_shape=jax.ShapeDtypeStruct((rows, cells), jnp.float32),
            in_specs=[pl.BlockSpec(memory_space=pltpu.HBM)] * 3,
            out_specs=pl.BlockSpec(memory_space=pltpu.VMEM),
            scratch_shapes=[
                pltpu.VMEM((2, 1, days), jnp.int32), sems((2,)),
                vmem((rows, cells)),
                vmem((CHUNKS, half, rows, c)),
                vmem((CHUNKS, GROUPS, c)),
                vmem((CHUNKS, GROUPS, c)),
                vmem((CHUNKS, half, rows, c)),
                sems, per_chunk, per_chunk, per_chunk, per_chunk,
                per_chunk, per_chunk,
                vmem((n, rows, direct)), vmem((n, rows, direct)),
                sems, sems, sems, sems,
            ],
            compiler_params=pltpu.CompilerParams(
                collective_id=0, has_side_effects=True, vmem_limit_bytes=36 * 2**20),
            name="anomaly",
        )(*(pltpu.with_memory_space_constraint(a, pltpu.HBM) for a in (
            thermal_field, seasonal_bucket.reshape(1, -1), season_of_record.reshape(1, -1))))

    placed = (P(("tm", "space"), None), P(), P())
    return jax.shard_map(
        shards, mesh=mesh, in_specs=placed, out_specs=P(("tm", "space"), None), check_vma=False
    )
```

profile of v0, /device:TPU:0, one launch (start us, length us, event | category | flops | bytes accessed | tf_op | source)
XLA Modules:
  0.0 42.1 jit_solution(16612529646077189146)
XLA Ops:
  0.0 41.2 %anomaly.1 = f32[4,49152]{1,0:T(4,128)S(1)} custom-call(f32[4,49152]{1,0:T(4,128)} %x_hbm.1, s32[1,128]{1,0:T(1,128)} %bitcast.2, s32[1,128]{1,0:T(1,128)} %bitcast.3), custom_call_target="tpu_custom_call" | custom-call | tf_op jit(solution)/shard_map/anomaly/pallas_call | solution.py:236
  41.3 0.9 %copy.5 = f32[4,49152]{1,0:T(4,128)} copy(f32[4,49152]{1,0:T(4,128)S(1)} %anomaly.1) | data formatting | bytes 1572864
where the time goes:
time: 42.3 us; the launch traced here: 42.1 us
  Pallas kernels  41.2 us (97%)
  local copies, waits for them, and re-layouts  0.88 us (2%)
    pallas_call x1, Pallas kernels, shards(): pl.pallas_call(functools.partial(kernel, nt, ns, CHUNKS, LAG, LEAD), out_...  41.2 us
    unnamed x1, local copies, waits for them, and re-layouts  0.88 us

commit v1 on v0

v1 whole, which is shorter than its diff:
```python
import functools

import jax
import jax.numpy as jnp
from jax import lax
from jax.experimental import pallas as pl
from jax.experimental.pallas import tpu as pltpu
from jax.sharding import PartitionSpec as P

GROUPS = 46
BASE_YEARS = 6
PLANES = 4
UNIT = 128
RAW = 12
SIZES = (2, 3, 3, 3, 3, 3, 3, 3, 3, 3, 3, 2, 2)
LAG = 2
RELAYS = 3
SPREAD = 3
SOLVE = 6
MESH = pl.DeviceIdType.MESH


def exact_dot(mask, x):
    high = x.astype(jnp.bfloat16)
    rest = x - high.astype(jnp.float32)
    middle = rest.astype(jnp.bfloat16)
    low = (rest - middle.astype(jnp.float32)).astype(jnp.bfloat16)
    total = jnp.dot(mask, low, preferred_element_type=jnp.float32)
    total += jnp.dot(mask, middle, preferred_element_type=jnp.float32)
    return total + jnp.dot(mask, high, preferred_element_type=jnp.float32)


def cuts(units, weights):
    total, edges = sum(weights), [0]
    for i in range(len(weights)):
        edge = units * sum(weights[:i + 1]) // total
        if edge > edges[-1]:
            edges.append(edge)
    return [(a * UNIT, (b - a) * UNIT) for a, b in zip(edges, edges[1:])]


def plan(nt, ns, cells):
    members = nt * (ns // PLANES)
    units = cells // members // UNIT
    raw = max(units * RAW // 48 // 2, 1)
    return members, raw * UNIT, (units - 2 * raw) * UNIT


def kernel(nt, ns, x_hbm, bucket_hbm, season_hbm, out_ref, calendar, xv, recv, sums, other, y,
           zin, fwd, gath, solved, zret, load_sem, date_sem, own_sem,
           send_a, recv_a, send_b, recv_b, send_s, recv_s, send_y, recv_y, send_o, recv_o,
           send_f, recv_f, send_z, recv_1, recv_2, recv_3, send_g, recv_g,
           send_h, recv_h, send_k, recv_k, send_v, recv_v):
    rows, cells = x_hbm.shape
    w = ns // PLANES
    members, e, mine = plan(nt, ns, cells)
    half = members * e
    start = 2 * half
    chunks = cuts(mine // UNIT, SIZES)
    relays = cuts(half // UNIT, (1,) * RELAYS)
    days = rows * nt * ns
    t, s = lax.axis_index("tm"), lax.axis_index("space")
    q = s // w
    j = s - q * w
    h = q // 2
    me = t * w + j
    mate = q + 1 - 2 * lax.rem(q, 2)
    across = 3 - q
    is_mid = (q == 1) | (q == 2)
    is_outer = jnp.logical_not(is_mid)
    mine_at = pl.multiple_of(start + me * mine, UNIT)
    here_at = pl.multiple_of(h * half, UNIT)
    there_at = pl.multiple_of((1 - h) * half, UNIT)

    def copy(src, dst, send, recv_sem, plane, place=None):
        pt, pj = (t, j) if place is None else place
        return pltpu.make_async_remote_copy(
            src_ref=src, dst_ref=dst, send_sem=send, recv_sem=recv_sem,
            device_id=(pt, plane * w + pj), device_id_type=MESH)

    def settle(ref, sem):
        pltpu.make_async_copy(ref, ref, sem).wait()

    def to_plane(body):
        for dj in range(w):
            for dt in range(nt):
                if dt == dj == 0:
                    continue
                pt, pj = lax.rem(t + dt, nt), lax.rem(j + dj, w)
                body(pt, pj, pt * w + pj)

    load = pltpu.make_async_copy(x_hbm, xv, load_sem)
    load.start()
    dates = [pltpu.make_async_copy(ref, calendar.at[i], date_sem.at[i])
             for i, ref in enumerate((bucket_hbm, season_hbm))]
    for date in dates:
        date.start()
    for k, (a, c) in enumerate(chunks):
        pltpu.make_async_copy(x_hbm.at[:, pl.ds(pl.multiple_of(mine_at + a, UNIT), c)],
                              recv.at[me, :, pl.ds(a, c)], recv_a.at[k]).start()

    @pl.when(is_mid)
    def _():
        pltpu.make_async_copy(x_hbm.at[:, pl.ds(here_at, half)], zin.at[0], own_sem).start()

    barrier = pltpu.get_barrier_semaphore()

    def greet(pt, plane, pj):
        pl.semaphore_signal(barrier, inc=1, device_id=(pt, plane * w + pj), device_id_type=MESH)

    to_plane(lambda pt, pj, p: greet(pt, q, pj))
    greet(t, mate, j)

    @pl.when(is_mid)
    def _():
        greet(t, across, j)
        pl.semaphore_wait(barrier, members + 1)

    @pl.when(is_outer)
    def _():
        pl.semaphore_wait(barrier, members)

    load.wait()

    def push(k):
        a, c = chunks[k]

        def one(pt, pj, p):
            copy(xv.at[:, pl.ds(pl.multiple_of(start + p * mine + a, UNIT), c)],
                 recv.at[me, :, pl.ds(a, c)], send_a, recv_a.at[k], q, (pt, pj)).start()
        to_plane(one)

    def back(k):
        a, c = chunks[k]
        at = pl.ds(pl.multiple_of(mine_at + a, UNIT), c)

        def one(pt, pj, p):
            copy(y.at[p, :, pl.ds(a, c)], out_ref.at[:, at], send_o, recv_o, q, (pt, pj)).start()
        to_plane(one)
        out_ref[:, at] = y[me, :, pl.ds(a, c)]

    def arrived(k):
        a, c = chunks[k]
        settle(recv.at[pl.ds(0, members), :, pl.ds(a, c)], recv_a.at[k])

    push(0)

    @pl.when(is_mid)
    def _():
        copy(xv.at[:, pl.ds(there_at, half)], zin.at[2], send_z, recv_2, across).start()
        for k in range(1, len(chunks)):
            push(k)
        for date in dates:
            date.wait()

        bucket, season = calendar[0], calendar[1]
        key = jnp.where(season < BASE_YEARS, bucket, -1)
        padded = sums.shape[0]

        def planned(count, plane_of):
            order = lax.broadcasted_iota(jnp.int32, (count, days), 0)
            plane, p = plane_of(order)
            day = ((p // w) * ns + plane * w + lax.rem(p, w)) * rows + lax.rem(order, rows)
            pick = day == lax.broadcasted_iota(jnp.int32, (count, days), 1)
            return lambda row: jnp.sum(jnp.where(pick, row, 0), axis=1, keepdims=True)

        here = 2 * members * rows
        of_half = planned(here, lambda order: (
            jnp.where(order < members * rows, q, mate),
            lax.rem(order, members * rows) // rows))
        member = of_half(bucket) == lax.broadcasted_iota(jnp.int32, (here, padded), 1)
        member = jnp.where(member, 1.0, 0.0).astype(jnp.bfloat16)
        key_row = jnp.broadcast_to(of_half(key), (here, here)).T[:1]
        group = lax.broadcasted_iota(jnp.int32, (padded, here), 0)
        baseline = jnp.where(group == key_row, 1.0, 0.0).astype(jnp.bfloat16)
        counted = lax.broadcasted_iota(jnp.int32, (padded, days), 0) == key
        counts = jnp.sum(jnp.where(counted, 1.0, 0.0), axis=1, keepdims=True)
        inverse = 1.0 / jnp.maximum(counts, 1.0)

        def slot_plane(order):
            slot = lax.rem(order // rows, 4)
            plane = jnp.where(slot == 0, q, jnp.where(slot == 1, mate,
                              jnp.where(slot == 2, across, 3 - mate)))
            return plane, order // (4 * rows)

        for i, (a, c) in enumerate(relays):
            settle(fwd.at[:, pl.ds(a, c)], recv_f.at[i])
            copy(fwd.at[:, pl.ds(a, c)], zin.at[3, :, pl.ds(a, c)], send_z, recv_3, across).start()

        def swap(k):
            a, c = chunks[k]
            return copy(sums.at[:, pl.ds(a, c)], other.at[:, pl.ds(a, c)], send_s, recv_s.at[k], across)

        def finish(k):
            a, c = chunks[k]
            cols = pl.ds(a, c)
            swap(k).wait_recv()
            climate = (sums[:, cols] + other[:, cols]) * inverse
            x = recv[:, :, cols].reshape(here, c)
            y[:, :, cols] = (x - exact_dot(member, climate)).reshape(2 * members, rows, c)
            high = pl.ds(members, members)
            copy(y.at[high, :, cols], y.at[pl.ds(0, members), :, cols], send_y, recv_y.at[k], mate).start()
            back(k)

        def spread():
            pltpu.make_async_copy(x_hbm.at[:, pl.ds(here_at, half)], zin.at[0], own_sem).wait()
            for i, sem in enumerate((recv_1, recv_2, recv_3)):
                settle(zin.at[i + 1], sem)

            def one(pt, pj, p):
                copy(zin.at[:, :, pl.ds(pl.multiple_of(p * e, UNIT), e)], gath.at[me],
                     send_g, recv_g, q, (pt, pj)).start()
            to_plane(one)
            gath[me] = zin[:, :, pl.ds(pl.multiple_of(me * e, UNIT), e)]

        def solve():
            of_all = planned(days, slot_plane)
            col = jnp.broadcast_to(of_all(bucket), (days, days))
            based = jnp.broadcast_to(of_all(key), (days, days)).T
            same = jnp.where(col == based, 1.0, 0.0)
            scale = 1.0 / jnp.sum(same, axis=1, keepdims=True)
            settle(gath.at[pl.ds(0, members - 1)], recv_g)
            x = gath[...].reshape(days, e)
            mean = exact_dot(same.astype(jnp.bfloat16), x) * scale
            solved[...] = (x - mean).reshape(members, 4, rows, e)
            at = pl.ds(pl.multiple_of(me * e, UNIT), e)
            out_at = pl.ds(pl.multiple_of(here_at + me * e, UNIT), e)

            def one(pt, pj, p):
                copy(solved.at[p, pl.ds(1, 3)], zret.at[:, :, at], send_h, recv_h, q, (pt, pj)).start()
            to_plane(one)

            def own(pt, pj, p):
                copy(solved.at[p, 0], out_ref.at[:, out_at], send_k, recv_k, q, (pt, pj)).start()
            to_plane(own)
            zret[:, :, at] = solved[me, pl.ds(1, 3)]
            out_ref[:, out_at] = solved[me, 0]

        def home():
            settle(gath.at[pl.ds(0, members - 1), pl.ds(1, 3)], recv_h)
            at = pl.ds(here_at, half)
            for i, plane in ((2, 3 - mate), (1, across), (0, mate)):
                copy(zret.at[i], out_ref.at[:, at], send_v, recv_v, plane).start()

        last = len(chunks) - 1
        for k in range(len(chunks)):
            if k == min(SPREAD, last):
                spread()
            if k == min(SOLVE, last):
                solve()
            arrived(k)
            a, c = chunks[k]
            settle(recv.at[pl.ds(members, members), :, pl.ds(a, c)], recv_b.at[k])
            sums[:, pl.ds(a, c)] = exact_dot(baseline, recv[:, :, pl.ds(a, c)].reshape(here, c))
            swap(k).start()
            if k == last:
                home()
            if k >= LAG:
                finish(k - LAG)
        for k in range(max(len(chunks) - LAG, 0), len(chunks)):
            finish(k)

        settle(sums, send_s)
        settle(y.at[pl.ds(members, members)], send_y)
        settle(zin.at[pl.ds(0, 2)], send_z)
        settle(gath.at[pl.ds(0, members - 1)], send_g)
        settle(gath.at[pl.ds(0, members - 1), pl.ds(1, 3)], send_h)
        settle(gath.at[pl.ds(0, members - 1), 0], send_k)
        settle(gath.at[pl.ds(0, members - 1), 0], recv_k)
        settle(zret, send_v)
        settle(fwd, recv_v)

    @pl.when(is_outer)
    def _():
        for i, (a, c) in enumerate(relays):
            copy(xv.at[:, pl.ds(pl.multiple_of(there_at + a, UNIT), c)], fwd.at[:, pl.ds(a, c)],
                 send_f, recv_f.at[i], mate).start()
        for k in range(1, len(chunks)):
            push(k)
        for k, (a, c) in enumerate(chunks):
            arrived(k)
            copy(recv.at[pl.ds(0, members), :, pl.ds(a, c)], recv.at[pl.ds(members, members), :, pl.ds(a, c)],
                 send_b, recv_b.at[k], mate).start()
            if k == 0:
                copy(xv.at[:, pl.ds(here_at, half)], zin.at[1], send_z, recv_1, mate).start()
        for k, (a, c) in enumerate(chunks):
            settle(y.at[pl.ds(0, members), :, pl.ds(a, c)], recv_y.at[k])
            back(k)

        for date in dates:
            date.wait()
        settle(fwd, send_f)
        settle(fwd, send_z)
        settle(recv.at[pl.ds(0, members)], send_b)
        settle(zin.at[pl.ds(0, 2)], recv_v)

    part = recv.at[pl.ds(0, members - 1)]
    settle(part, send_a)
    settle(part, recv_o)
    settle(part, send_o)


def solution(mesh):
    nt, ns = mesh.shape["tm"], mesh.shape["space"]

    def shards(thermal_field, seasonal_bucket, season_of_record):
        rows, cells = thermal_field.shape
        members, e, mine = plan(nt, ns, cells)
        days, half = rows * nt * ns, members * e
        count = len(cuts(mine // UNIT, SIZES))
        sems = pltpu.SemaphoreType.DMA
        per_chunk = sems((count,))
        vmem = functools.partial(pltpu.VMEM, dtype=jnp.float32)
        return pl.pallas_call(
            functools.partial(kernel, nt, ns),
            out_shape=jax.ShapeDtypeStruct((rows, cells), jnp.float32),
            in_specs=[pl.BlockSpec(memory_space=pltpu.HBM)] * 3,
            out_specs=pl.BlockSpec(memory_space=pltpu.VMEM),
            scratch_shapes=[
                pltpu.VMEM((2, 1, days), jnp.int32),
                vmem((rows, cells)),
                vmem((2 * members, rows, mine)),
                vmem((GROUPS, mine)),
                vmem((GROUPS, mine)),
                vmem((2 * members, rows, mine)),
                vmem((4, rows, half)), vmem((rows, half)),
                vmem((members, 4, rows, e)), vmem((members, 4, rows, e)), vmem((3, rows, half)),
                sems, sems((2,)), sems,
                sems, per_chunk, sems, per_chunk, sems, per_chunk, sems, per_chunk, sems, sems,
                sems, sems((RELAYS,)), sems, sems, sems, sems, sems, sems,
                sems, sems, sems, sems, sems, sems,
            ],
            compiler_params=pltpu.CompilerParams(
                collective_id=0, has_side_effects=True, vmem_limit_bytes=56 * 2**20),
            name="anomaly",
        )(*(pltpu.with_memory_space_constraint(a, pltpu.HBM) for a in (
            thermal_field, seasonal_bucket.reshape(1, -1), season_of_record.reshape(1, -1))))

    placed = (P(("tm", "space"), None), P(), P())
    return jax.shard_map(
        shards, mesh=mesh, in_specs=placed, out_specs=P(("tm", "space"), None), check_vma=False
    )
```

time: 42.3 us -> 47.7 us (1.13)
  Pallas kernels: 41.2 us -> 45.5 us
  local copies, waits for them, and re-layouts: 0.88 us -> 2.06 us
    pallas_call x1, Pallas kernels: 41.2 us -> 45.5 us  [shards(): pl.pallas_call(functools.partial(kernel, nt, ns), out_shape=jax.ShapeDtyp...]
    unnamed x1, local copies, waits for them, and re-layouts: 0.88 us -> 2.06 us
where the time goes in v1:
time: 47.7 us; the launch traced here: 47.6 us
  Pallas kernels  45.5 us (95%)
  local copies, waits for them, and re-layouts  2.06 us (4%)
    pallas_call x1, Pallas kernels, shards(): pl.pallas_call(functools.partial(kernel, nt, ns), out_shape=jax.ShapeDtyp...  45.5 us
    unnamed x1, local copies, waits for them, and re-layouts  2.06 us

profile of v1, /device:TPU:0, one launch (start us, length us, event | category | flops | bytes accessed | tf_op | source)
XLA Modules:
  0.0 47.6 jit_solution(4564148752923510537)
XLA Ops:
  0.0 45.5 %anomaly.1 = f32[4,49152]{1,0:T(4,128)} custom-call(f32[4,49152]{1,0:T(4,128)} %x_hbm.1, s32[1,128]{1,0:T(1,128)} %bitcast.2, s32[1,128]{1,0:T(1,128)} %bitcast.3), custom_call_target="tpu_custom_call" | custom-call | tf_op jit(solution)/shard_map/anomaly/pallas_call | solution.py:314
  45.5 2.1 %copy.5 = f32[4,49152]{1,0:T(4,128)} copy(f32[4,49152]{1,0:T(4,128)} %anomaly.1) | data formatting | bytes 1572864

commit v2 on v1

--- a/solution.py
+++ b/solution.py
@@ -13,10 +13,14 @@
 UNIT = 128
 RAW = 12
 SIZES = (2, 3, 3, 3, 3, 3, 3, 3, 3, 3, 3, 2, 2)
-LAG = 2
-RELAYS = 3
-SPREAD = 3
-SOLVE = 6
+LAG = 3
+RELAY = 2
+AHEAD = 20
+FORWARD = 3
+SPREAD = 5
+SOLVE = 9
+OWN = 3
+DIRECT = 2
 MESH = pl.DeviceIdType.MESH
 
 
@@ -47,17 +51,17 @@
 
 
 def kernel(nt, ns, x_hbm, bucket_hbm, season_hbm, out_ref, calendar, xv, recv, sums, other, y,
-           zin, fwd, gath, solved, zret, load_sem, date_sem, own_sem,
-           send_a, recv_a, send_b, recv_b, send_s, recv_s, send_y, recv_y, send_o, recv_o,
+           zin, fwd, gath, solved, load_sem, date_sem, own_sem,
+           send_a, recv_a, send_b, recv_b, send_s, recv_s, send_o, recv_o,
            send_f, recv_f, send_z, recv_1, recv_2, recv_3, send_g, recv_g,
-           send_h, recv_h, send_k, recv_k, send_v, recv_v):
+           send_k, recv_k, send_v, recv_v):
     rows, cells = x_hbm.shape
     w = ns // PLANES
     members, e, mine = plan(nt, ns, cells)
     half = members * e
     start = 2 * half
     chunks = cuts(mine // UNIT, SIZES)
-    relays = cuts(half // UNIT, (1,) * RELAYS)
+    direct = min(DIRECT, len(chunks) - 1)
     days = rows * nt * ns
     t, s = lax.axis_index("tm"), lax.axis_index("space")
     q = s // w
@@ -81,10 +85,10 @@
     def settle(ref, sem):
         pltpu.make_async_copy(ref, ref, sem).wait()
 
-    def to_plane(body):
+    def to_plane(body, own=False):
         for dj in range(w):
             for dt in range(nt):
-                if dt == dj == 0:
+                if dt == dj == 0 and not own:
                     continue
                 pt, pj = lax.rem(t + dt, nt), lax.rem(j + dj, w)
                 body(pt, pj, pt * w + pj)
@@ -95,12 +99,18 @@
              for i, ref in enumerate((bucket_hbm, season_hbm))]
     for date in dates:
         date.start()
-    for k, (a, c) in enumerate(chunks):
+
+    def keep(k):
+        a, c = chunks[k]
         pltpu.make_async_copy(x_hbm.at[:, pl.ds(pl.multiple_of(mine_at + a, UNIT), c)],
                               recv.at[me, :, pl.ds(a, c)], recv_a.at[k]).start()
+    for k in range(direct, len(chunks)):
+        keep(k)
 
     @pl.when(is_mid)
     def _():
+        for k in range(direct):
+            keep(k)
         pltpu.make_async_copy(x_hbm.at[:, pl.ds(here_at, half)], zin.at[0], own_sem).start()
 
     barrier = pltpu.get_barrier_semaphore()
@@ -109,16 +119,16 @@
         pl.semaphore_signal(barrier, inc=1, device_id=(pt, plane * w + pj), device_id_type=MESH)
 
     to_plane(lambda pt, pj, p: greet(pt, q, pj))
-    greet(t, mate, j)
 
     @pl.when(is_mid)
     def _():
+        to_plane(lambda pt, pj, p: greet(pt, mate, pj), True)
         greet(t, across, j)
-        pl.semaphore_wait(barrier, members + 1)
+        pl.semaphore_wait(barrier, members)
 
     @pl.when(is_outer)
     def _():
-        pl.semaphore_wait(barrier, members)
+        pl.semaphore_wait(barrier, 2 * members - 1)
 
     load.wait()
 
@@ -134,21 +144,24 @@
         a, c = chunks[k]
         at = pl.ds(pl.multiple_of(mine_at + a, UNIT), c)
 
-        def one(pt, pj, p):
+        def far(pt, pj, p):
+            copy(y.at[members + p, :, pl.ds(a, c)], out_ref.at[:, at], send_o, recv_o, mate, (pt, pj)).start()
+
+        def near(pt, pj, p):
             copy(y.at[p, :, pl.ds(a, c)], out_ref.at[:, at], send_o, recv_o, q, (pt, pj)).start()
-        to_plane(one)
+        to_plane(far, True)
+        to_plane(near)
         out_ref[:, at] = y[me, :, pl.ds(a, c)]
 
     def arrived(k):
         a, c = chunks[k]
         settle(recv.at[pl.ds(0, members), :, pl.ds(a, c)], recv_a.at[k])
 
-    push(0)
-
     @pl.when(is_mid)
     def _():
+        push(0)
         copy(xv.at[:, pl.ds(there_at, half)], zin.at[2], send_z, recv_2, across).start()
-        for k in range(1, len(chunks)):
+        for k in range(1, min(AHEAD, len(chunks))):
             push(k)
         for date in dates:
             date.wait()
@@ -183,9 +196,9 @@
                               jnp.where(slot == 2, across, 3 - mate)))
             return plane, order // (4 * rows)
 
-        for i, (a, c) in enumerate(relays):
-            settle(fwd.at[:, pl.ds(a, c)], recv_f.at[i])
-            copy(fwd.at[:, pl.ds(a, c)], zin.at[3, :, pl.ds(a, c)], send_z, recv_3, across).start()
+        def relay():
+            settle(fwd, recv_f)
+            copy(fwd, zin.at[3], send_z, recv_3, across).start()
 
         def swap(k):
             a, c = chunks[k]
@@ -198,8 +211,6 @@
             climate = (sums[:, cols] + other[:, cols]) * inverse
             x = recv[:, :, cols].reshape(here, c)
             y[:, :, cols] = (x - exact_dot(member, climate)).reshape(2 * members, rows, c)
-            high = pl.ds(members, members)
-            copy(y.at[high, :, cols], y.at[pl.ds(0, members), :, cols], send_y, recv_y.at[k], mate).start()
             back(k)
 
         def spread():
@@ -212,6 +223,13 @@
                      send_g, recv_g, q, (pt, pj)).start()
             to_plane(one)
             gath[me] = zin[:, :, pl.ds(pl.multiple_of(me * e, UNIT), e)]
+
+        solved_at = pl.ds(pl.multiple_of(here_at + me * e, UNIT), e)
+
+        def send_home(slot, plane, own, send, recv_sem):
+            def one(pt, pj, p):
+                copy(solved.at[p, slot], out_ref.at[:, solved_at], send, recv_sem, plane, (pt, pj)).start()
+            to_plane(one, own)
 
         def solve():
             of_all = planned(days, slot_plane)
@@ -223,27 +241,16 @@
             x = gath[...].reshape(days, e)
             mean = exact_dot(same.astype(jnp.bfloat16), x) * scale
             solved[...] = (x - mean).reshape(members, 4, rows, e)
-            at = pl.ds(pl.multiple_of(me * e, UNIT), e)
-            out_at = pl.ds(pl.multiple_of(here_at + me * e, UNIT), e)
-
-            def one(pt, pj, p):
-                copy(solved.at[p, pl.ds(1, 3)], zret.at[:, :, at], send_h, recv_h, q, (pt, pj)).start()
-            to_plane(one)
-
-            def own(pt, pj, p):
-                copy(solved.at[p, 0], out_ref.at[:, out_at], send_k, recv_k, q, (pt, pj)).start()
-            to_plane(own)
-            zret[:, :, at] = solved[me, pl.ds(1, 3)]
-            out_ref[:, out_at] = solved[me, 0]
-
-        def home():
-            settle(gath.at[pl.ds(0, members - 1), pl.ds(1, 3)], recv_h)
-            at = pl.ds(here_at, half)
-            for i, plane in ((2, 3 - mate), (1, across), (0, mate)):
-                copy(zret.at[i], out_ref.at[:, at], send_v, recv_v, plane).start()
+            send_home(1, mate, True, send_k, recv_k)
+            send_home(0, q, False, send_k, recv_k)
+            out_ref[:, solved_at] = solved[me, 0]
 
         last = len(chunks) - 1
         for k in range(len(chunks)):
+            if k + AHEAD < len(chunks):
+                push(k + AHEAD)
+            if k == min(RELAY, last):
+                relay()
             if k == min(SPREAD, last):
                 spread()
             if k == min(SOLVE, last):
@@ -254,50 +261,52 @@
             sums[:, pl.ds(a, c)] = exact_dot(baseline, recv[:, :, pl.ds(a, c)].reshape(here, c))
             swap(k).start()
             if k == last:
-                home()
+                send_home(3, 3 - mate, True, send_v, recv_v)
+                send_home(2, across, True, send_v, recv_v)
             if k >= LAG:
                 finish(k - LAG)
         for k in range(max(len(chunks) - LAG, 0), len(chunks)):
             finish(k)
 
         settle(sums, send_s)
-        settle(y.at[pl.ds(members, members)], send_y)
         settle(zin.at[pl.ds(0, 2)], send_z)
         settle(gath.at[pl.ds(0, members - 1)], send_g)
-        settle(gath.at[pl.ds(0, members - 1), pl.ds(1, 3)], send_h)
+        settle(gath.at[:, 0], send_k)
         settle(gath.at[pl.ds(0, members - 1), 0], send_k)
         settle(gath.at[pl.ds(0, members - 1), 0], recv_k)
-        settle(zret, send_v)
-        settle(fwd, recv_v)
+        settle(gath.at[:, pl.ds(0, 2)], send_v)
+        settle(y.at[pl.ds(0, 2 * members - 1)], send_o)
+        settle(recv.at[pl.ds(0, members - 1)], recv_o)
+        settle(recv.at[pl.ds(0, members - 1)], send_a)
 
     @pl.when(is_outer)
     def _():
-        for i, (a, c) in enumerate(relays):
-            copy(xv.at[:, pl.ds(pl.multiple_of(there_at + a, UNIT), c)], fwd.at[:, pl.ds(a, c)],
-                 send_f, recv_f.at[i], mate).start()
-        for k in range(1, len(chunks)):
+        for k, (a, c) in enumerate(chunks[:direct]):
+            def one(pt, pj, p):
+                copy(xv.at[:, pl.ds(pl.multiple_of(start + p * mine + a, UNIT), c)],
+                     recv.at[members + me, :, pl.ds(a, c)], send_b, recv_b.at[k], mate, (pt, pj)).start()
+            to_plane(one, True)
+            if k == min(FORWARD, direct - 1):
+                copy(xv.at[:, pl.ds(there_at, half)], fwd, send_f, recv_f, mate).start()
+        for k in range(direct, len(chunks)):
             push(k)
-        for k, (a, c) in enumerate(chunks):
+        for k in range(direct, len(chunks)):
+            a, c = chunks[k]
             arrived(k)
             copy(recv.at[pl.ds(0, members), :, pl.ds(a, c)], recv.at[pl.ds(members, members), :, pl.ds(a, c)],
                  send_b, recv_b.at[k], mate).start()
-            if k == 0:
+            if k == max(direct, min(OWN, len(chunks) - 1)):
                 copy(xv.at[:, pl.ds(here_at, half)], zin.at[1], send_z, recv_1, mate).start()
-        for k, (a, c) in enumerate(chunks):
-            settle(y.at[pl.ds(0, members), :, pl.ds(a, c)], recv_y.at[k])
-            back(k)
-
         for date in dates:
             date.wait()
         settle(fwd, send_f)
         settle(fwd, send_z)
         settle(recv.at[pl.ds(0, members)], send_b)
-        settle(zin.at[pl.ds(0, 2)], recv_v)
-
-    part = recv.at[pl.ds(0, members - 1)]
-    settle(part, send_a)
-    settle(part, recv_o)
-    settle(part, send_o)
+        settle(recv.at[pl.ds(0, members - 1), :, pl.ds(chunks[direct][0], mine - chunks[direct][0])], send_a)
+        settle(gath.at[:, 0], recv_k)
+        settle(recv.at[pl.ds(0, members)], recv_o)
+
+    settle(fwd, recv_v)
 
 
 def solution(mesh):
@@ -324,14 +333,14 @@
                 vmem((GROUPS, mine)),
                 vmem((2 * members, rows, mine)),
                 vmem((4, rows, half)), vmem((rows, half)),
-                vmem((members, 4, rows, e)), vmem((members, 4, rows, e)), vmem((3, rows, half)),
+                vmem((members, 4, rows, e)), vmem((members, 4, rows, e)),
                 sems, sems((2,)), sems,
-                sems, per_chunk, sems, per_chunk, sems, per_chunk, sems, per_chunk, sems, sems,
-                sems, sems((RELAYS,)), sems, sems, sems, sems, sems, sems,
-                sems, sems, sems, sems, sems, sems,
+                sems, per_chunk, sems, per_chunk, sems, per_chunk, sems, sems,
+                sems, sems, sems, sems, sems, sems, sems, sems,
+                sems, sems, sems, sems,
             ],
             compiler_params=pltpu.CompilerParams(
-                collective_id=0, has_side_effects=True, vmem_limit_bytes=56 * 2**20),
+                collective_id=0, has_side_effects=True, vmem_limit_bytes=30 * 2**20),
             name="anomaly",
         )(*(pltpu.with_memory_space_constraint(a, pltpu.HBM) for a in (
             thermal_field, seasonal_bucket.reshape(1, -1), season_of_record.reshape(1, -1))))

time: 47.7 us -> 39.7 us (0.83)
  Pallas kernels: 45.5 us -> 38.6 us
  local copies, waits for them, and re-layouts: 2.06 us -> 0.88 us
    pallas_call x1, Pallas kernels: 45.5 us -> 38.6 us  [shards(): pl.pallas_call(functools.partial(kernel, nt, ns), out_shape=jax.ShapeDtyp...]
    unnamed x1, local copies, waits for them, and re-layouts: 2.06 us -> 0.88 us
where the time goes in v2:
time: 39.7 us; the launch traced here: 39.5 us
  Pallas kernels  38.6 us (97%)
  local copies, waits for them, and re-layouts  0.88 us (2%)
    pallas_call x1, Pallas kernels, shards(): pl.pallas_call(functools.partial(kernel, nt, ns), out_shape=jax.ShapeDtyp...  38.6 us
    unnamed x1, local copies, waits for them, and re-layouts  0.88 us

profile of v2, /device:TPU:0, one launch (start us, length us, event | category | flops | bytes accessed | tf_op | source)
XLA Modules:
  0.0 39.5 jit_solution(330883546560672224)
XLA Ops:
  0.0 38.6 %anomaly.1 = f32[4,49152]{1,0:T(4,128)S(1)} custom-call(f32[4,49152]{1,0:T(4,128)} %x_hbm.1, s32[1,128]{1,0:T(1,128)} %bitcast.2, s32[1,128]{1,0:T(1,128)} %bitcast.3), custom_call_target="tpu_custom_call" | custom-call | tf_op jit(solution)/shard_map/anomaly/pallas_call | solution.py:323
  38.7 0.9 %copy.5 = f32[4,49152]{1,0:T(4,128)} copy(f32[4,49152]{1,0:T(4,128)S(1)} %anomaly.1) | data formatting | bytes 1572864

commit v3 on v2

v3 whole, which is shorter than its diff:
```python
import functools

import jax
import jax.numpy as jnp
from jax import lax
from jax.experimental import pallas as pl
from jax.experimental.pallas import tpu as pltpu
from jax.sharding import PartitionSpec as P

GROUPS = 46
BASE_YEARS = 6
PLANES = 4
UNIT = 128
RAW = 8
SIZES = (2, 3, 3, 3, 3, 3, 3, 3, 3, 3, 3, 2, 2)
PIECES = 4
DIRECT = 2
LAG = 3
RAW_SENT = 0
RAW_FROM = 5
RAW_EVERY = 2
MESH = pl.DeviceIdType.MESH


def exact_dot(mask, x):
    high = x.astype(jnp.bfloat16)
    rest = x - high.astype(jnp.float32)
    middle = rest.astype(jnp.bfloat16)
    low = (rest - middle.astype(jnp.float32)).astype(jnp.bfloat16)
    total = jnp.dot(mask, low, preferred_element_type=jnp.float32)
    total += jnp.dot(mask, middle, preferred_element_type=jnp.float32)
    return total + jnp.dot(mask, high, preferred_element_type=jnp.float32)


def cuts(start, units, weights):
    total, edges = sum(weights), [0]
    for i in range(len(weights)):
        edge = units * sum(weights[:i + 1]) // total
        if edge > edges[-1]:
            edges.append(edge)
    return [(start + a * UNIT, (b - a) * UNIT) for a, b in zip(edges, edges[1:])]


def plan(nt, ns, cells):
    members = nt * (ns // PLANES)
    units = cells // members // UNIT
    raw = max(units * RAW // 48, 1)
    swapped = cuts(0, units - raw, SIZES)
    return members, units * UNIT, raw * UNIT, swapped, cuts((units - raw) * UNIT, raw, (1,) * PIECES)


def kernel(nt, ns, x_hbm, bucket_hbm, season_hbm, out_ref, calendar, xv, recv, sums, other, y, far,
           load_sem, date_sem, send_a, recv_a, send_b, recv_b, send_s, recv_s, send_o, recv_o,
           send_r, recv_r):
    rows, cells = x_hbm.shape
    w = ns // PLANES
    members, mine, e, swapped, raws = plan(nt, ns, cells)
    chunks = swapped + raws
    last = len(swapped) - 1
    order = []
    for k in range(len(swapped)):
        order.append(k)
        order += [len(swapped) + i for i in range(len(raws))
                  if min(RAW_FROM + i * RAW_EVERY, last) == k]
    direct = min(DIRECT, len(swapped) - 1)
    days = rows * nt * ns
    t, s = lax.axis_index("tm"), lax.axis_index("space")
    q = s // w
    j = s - q * w
    me = t * w + j
    mate = q + 1 - 2 * lax.rem(q, 2)
    across = 3 - q
    beyond = 3 - mate
    is_mid = (q == 1) | (q == 2)
    is_outer = jnp.logical_not(is_mid)
    mine_at = pl.multiple_of(me * mine, UNIT)

    def copy(src, dst, send, recv_sem, plane, place):
        pt, pj = place
        return pltpu.make_async_remote_copy(
            src_ref=src, dst_ref=dst, send_sem=send, recv_sem=recv_sem,
            device_id=(pt, plane * w + pj), device_id_type=MESH)

    def settle(ref, sem):
        pltpu.make_async_copy(ref, ref, sem).wait()

    def to_plane(body, own=False):
        for dj in range(w):
            for dt in range(nt):
                if dt == dj == 0 and not own:
                    continue
                pt, pj = lax.rem(t + dt, nt), lax.rem(j + dj, w)
                body(pt, pj, pt * w + pj)

    load = pltpu.make_async_copy(x_hbm, xv, load_sem)
    load.start()
    barrier = pltpu.get_barrier_semaphore()

    def greet(plane, own):
        def one(pt, pj, p):
            pl.semaphore_signal(barrier, inc=1, device_id=(pt, plane * w + pj), device_id_type=MESH)
        to_plane(one, own)

    greet(q, False)

    @pl.when(is_mid)
    def _():
        for plane in (across, mate, beyond):
            greet(plane, True)

    dates = [pltpu.make_async_copy(ref, calendar.at[i], date_sem.at[i])
             for i, ref in enumerate((bucket_hbm, season_hbm))]

    def keep(k):
        a, c = chunks[k]
        pltpu.make_async_copy(x_hbm.at[:, pl.ds(pl.multiple_of(mine_at + a, UNIT), c)],
                              recv.at[me, :, pl.ds(a, c)], recv_a.at[k]).start()

    for k in order[direct:]:
        keep(k)

    def part(p, a, c):
        return xv.at[:, pl.ds(pl.multiple_of(p * mine + a, UNIT), c)]

    def push(k):
        a, c = chunks[k]

        def one(pt, pj, p):
            copy(part(p, a, c), recv.at[me, :, pl.ds(a, c)], send_a, recv_a.at[k], q, (pt, pj)).start()
        to_plane(one)

    def arrived(k):
        a, c = chunks[k]
        settle(recv.at[pl.ds(0, members), :, pl.ds(a, c)], recv_a.at[k])

    def send_raw(plane, slot):
        def one(pt, pj, p):
            copy(part(p, mine - e, e), far.at[slot], send_r, recv_r, plane, (pt, pj)).start()
        to_plane(one, True)

    @pl.when(is_mid)
    def _():
        for k in range(direct):
            keep(k)
        for date in dates:
            date.start()
        pl.semaphore_wait(barrier, 2 * members - 1)
        load.wait()
        push(0)
        send_raw(across, me)
        for k in order[1:]:
            push(k)
        for date in dates:
            date.wait()

        bucket, season = calendar[0], calendar[1]
        key = jnp.where(season < BASE_YEARS, bucket, -1)
        padded = sums.shape[0]
        here = 2 * members * rows

        def half(first, second):
            order = lax.broadcasted_iota(jnp.int32, (here, days), 0)
            plane = jnp.where(order < members * rows, first, second)
            p = lax.rem(order, members * rows) // rows
            day = ((p // w) * ns + plane * w + lax.rem(p, w)) * rows + lax.rem(order, rows)
            pick = day == lax.broadcasted_iota(jnp.int32, (here, days), 1)
            return lambda row: jnp.sum(jnp.where(pick, row, 0), axis=1, keepdims=True)

        def baseline(of_half):
            key_row = jnp.broadcast_to(of_half(key), (here, here)).T[:1]
            group = lax.broadcasted_iota(jnp.int32, (padded, here), 0)
            return jnp.where(group == key_row, 1.0, 0.0).astype(jnp.bfloat16)

        ours = half(q, mate)
        member = ours(bucket) == lax.broadcasted_iota(jnp.int32, (here, padded), 1)
        member = jnp.where(member, 1.0, 0.0).astype(jnp.bfloat16)
        of_ours, of_theirs = baseline(ours), baseline(half(across, beyond))
        counted = lax.broadcasted_iota(jnp.int32, (padded, days), 0) == key
        counts = jnp.sum(jnp.where(counted, 1.0, 0.0), axis=1, keepdims=True)
        inverse = 1.0 / jnp.maximum(counts, 1.0)

        def total(k):
            a, c = chunks[k]
            arrived(k)
            settle(recv.at[pl.ds(members, members), :, pl.ds(a, c)], recv_b.at[k])
            return exact_dot(of_ours, recv[:, :, pl.ds(a, c)].reshape(here, c))

        def swap(k):
            a, c = chunks[k]
            return copy(sums.at[:, pl.ds(a, c)], other.at[:, pl.ds(a, c)], send_s, recv_s.at[k], across, (t, j))

        def back(k, both):
            a, c = chunks[k]
            cols = pl.ds(a, c)
            at = pl.ds(pl.multiple_of(mine_at + a, UNIT), c)
            x = recv[:, :, cols].reshape(here, c)
            y[:, :, cols] = (x - exact_dot(member, both * inverse)).reshape(2 * members, rows, c)

            def outer(pt, pj, p):
                copy(y.at[members + p, :, cols], out_ref.at[:, at], send_o, recv_o, mate, (pt, pj)).start()

            def near(pt, pj, p):
                copy(y.at[p, :, cols], out_ref.at[:, at], send_o, recv_o, q, (pt, pj)).start()
            to_plane(outer, True)
            to_plane(near)
            out_ref[:, at] = y[me, :, cols]

        def finish(k):
            a, c = chunks[k]
            swap(k).wait_recv()
            back(k, sums[:, pl.ds(a, c)] + other[:, pl.ds(a, c)])

        def finish_raw(k):
            a, c = chunks[k]
            if k == len(swapped):
                settle(far, recv_r)
            theirs = far[:, :, pl.ds(a - (mine - e), c)].reshape(here, c)
            back(k, total(k) + exact_dot(of_theirs, theirs))

        for k in order:
            if k > last:
                finish_raw(k)
                continue
            a, c = chunks[k]
            sums[:, pl.ds(a, c)] = total(k)
            swap(k).start()
            if k >= LAG:
                finish(k - LAG)
        for k in range(max(len(swapped) - LAG, 0), len(swapped)):
            finish(k)

        settle(sums, send_s)
        settle(far.at[pl.ds(0, members)], send_r)
        settle(y.at[pl.ds(0, 2 * members - 1)], send_o)
        settle(recv.at[pl.ds(0, members - 1)], recv_o)
        settle(recv.at[pl.ds(0, members - 1)], send_a)

    @pl.when(is_outer)
    def _():
        pl.semaphore_wait(barrier, 3 * members - 1)
        load.wait()
        for k, (a, c) in enumerate(chunks[:direct]):
            def one(pt, pj, p):
                copy(part(p, a, c), recv.at[members + me, :, pl.ds(a, c)],
                     send_b, recv_b.at[k], mate, (pt, pj)).start()
            to_plane(one, True)
        for k in order[direct:]:
            push(k)
        for i, k in enumerate(order[direct:]):
            a, c = chunks[k]
            if i == min(RAW_SENT, last - direct):
                send_raw(beyond, members + me)
            arrived(k)
            copy(recv.at[pl.ds(0, members), :, pl.ds(a, c)], recv.at[pl.ds(members, members), :, pl.ds(a, c)],
                 send_b, recv_b.at[k], mate, (t, j)).start()
        settle(far.at[pl.ds(0, members)], send_r)
        settle(recv.at[pl.ds(0, members)], send_b)
        settle(recv.at[pl.ds(0, members - 1), :, pl.ds(chunks[direct][0], mine - chunks[direct][0])], send_a)
        settle(recv.at[pl.ds(0, members)], recv_o)


def solution(mesh):
    nt, ns = mesh.shape["tm"], mesh.shape["space"]

    def shards(thermal_field, seasonal_bucket, season_of_record):
        rows, cells = thermal_field.shape
        members, mine, e, swapped, raws = plan(nt, ns, cells)
        days = rows * nt * ns
        sems = pltpu.SemaphoreType.DMA
        per_chunk, per_swap = sems((len(swapped) + len(raws),)), sems((len(swapped),))
        vmem = functools.partial(pltpu.VMEM, dtype=jnp.float32)
        return pl.pallas_call(
            functools.partial(kernel, nt, ns),
            out_shape=jax.ShapeDtypeStruct((rows, cells), jnp.float32),
            in_specs=[pl.BlockSpec(memory_space=pltpu.HBM)] * 3,
            out_specs=pl.BlockSpec(memory_space=pltpu.VMEM),
            scratch_shapes=[
                pltpu.VMEM((2, 1, days), jnp.int32),
                vmem((rows, cells)),
                vmem((2 * members, rows, mine)),
                vmem((GROUPS, mine - e)),
                vmem((GROUPS, mine - e)),
                vmem((2 * members, rows, mine)),
                vmem((2 * members, rows, e)),
                sems, sems((2,)),
                sems, per_chunk, sems, per_chunk, sems, per_swap, sems, sems,
                sems, sems,
            ],
            compiler_params=pltpu.CompilerParams(
                collective_id=0, has_side_effects=True, vmem_limit_bytes=30 * 2**20),
            name="anomaly",
        )(*(pltpu.with_memory_space_constraint(a, pltpu.HBM) for a in (
            thermal_field, seasonal_bucket.reshape(1, -1), season_of_record.reshape(1, -1))))

    placed = (P(("tm", "space"), None), P(), P())
    return jax.shard_map(
        shards, mesh=mesh, in_specs=placed, out_specs=P(("tm", "space"), None), check_vma=False
    )
```

time: 39.7 us -> 38.7 us (0.975)
  Pallas kernels: 38.6 us -> 37.7 us
    pallas_call x1, Pallas kernels: 38.6 us -> 37.7 us  [shards(): pl.pallas_call(functools.partial(kernel, nt, ns), out_shape=jax.ShapeDtyp...]
where the time goes in v3:
time: 38.7 us; the launch traced here: 38.6 us
  Pallas kernels  37.7 us (97%)
  local copies, waits for them, and re-layouts  0.88 us (2%)
    pallas_call x1, Pallas kernels, shards(): pl.pallas_call(functools.partial(kernel, nt, ns), out_shape=jax.ShapeDtyp...  37.7 us
    unnamed x1, local copies, waits for them, and re-layouts  0.88 us

profile of v3, /device:TPU:0, one launch (start us, length us, event | category | flops | bytes accessed | tf_op | source)
XLA Modules:
  0.0 38.6 jit_solution(7520622018044946202)
XLA Ops:
  0.0 37.7 %anomaly.1 = f32[4,49152]{1,0:T(4,128)S(1)} custom-call(f32[4,49152]{1,0:T(4,128)} %x_hbm.1, s32[1,128]{1,0:T(1,128)} %bitcast.2, s32[1,128]{1,0:T(1,128)} %bitcast.3), custom_call_target="tpu_custom_call" | custom-call | tf_op jit(solution)/shard_map/anomaly/pallas_call | solution.py:272
  37.7 0.9 %copy.5 = f32[4,49152]{1,0:T(4,128)} copy(f32[4,49152]{1,0:T(4,128)S(1)} %anomaly.1) | data formatting | bytes 1572864

commit v4 on v3

--- a/solution.py
+++ b/solution.py
@@ -12,7 +12,7 @@
 PLANES = 4
 UNIT = 128
 RAW = 8
-SIZES = (2, 3, 3, 3, 3, 3, 3, 3, 3, 3, 3, 2, 2)
+SIZES = (2, 3, 3, 4, 4, 4, 4, 4, 4, 3, 2, 1)
 PIECES = 4
 DIRECT = 2
 LAG = 3
@@ -50,7 +50,7 @@
 
 
 def kernel(nt, ns, x_hbm, bucket_hbm, season_hbm, out_ref, calendar, xv, recv, sums, other, y, far,
-           load_sem, date_sem, send_a, recv_a, send_b, recv_b, send_s, recv_s, send_o, recv_o,
+           load_sem, date_sem, send_a, recv_a, send_b, send_s, recv_s, send_o, recv_o,
            send_r, recv_r):
     rows, cells = x_hbm.shape
     w = ns // PLANES
@@ -129,10 +129,6 @@
             copy(part(p, a, c), recv.at[me, :, pl.ds(a, c)], send_a, recv_a.at[k], q, (pt, pj)).start()
         to_plane(one)
 
-    def arrived(k):
-        a, c = chunks[k]
-        settle(recv.at[pl.ds(0, members), :, pl.ds(a, c)], recv_a.at[k])
-
     def send_raw(plane, slot):
         def one(pt, pj, p):
             copy(part(p, mine - e, e), far.at[slot], send_r, recv_r, plane, (pt, pj)).start()
@@ -181,8 +177,7 @@
 
         def total(k):
             a, c = chunks[k]
-            arrived(k)
-            settle(recv.at[pl.ds(members, members), :, pl.ds(a, c)], recv_b.at[k])
+            settle(recv.at[:, :, pl.ds(a, c)], recv_a.at[k])
             return exact_dot(of_ours, recv[:, :, pl.ds(a, c)].reshape(here, c))
 
         def swap(k):
@@ -196,12 +191,11 @@
             x = recv[:, :, cols].reshape(here, c)
             y[:, :, cols] = (x - exact_dot(member, both * inverse)).reshape(2 * members, rows, c)
 
-            def outer(pt, pj, p):
-                copy(y.at[members + p, :, cols], out_ref.at[:, at], send_o, recv_o, mate, (pt, pj)).start()
+            for p in range(members):
+                copy(y.at[members + p, :, cols], out_ref.at[:, at], send_o, recv_o, mate, (p // w, p % w)).start()
 
             def near(pt, pj, p):
                 copy(y.at[p, :, cols], out_ref.at[:, at], send_o, recv_o, q, (pt, pj)).start()
-            to_plane(outer, True)
             to_plane(near)
             out_ref[:, at] = y[me, :, cols]
 
@@ -242,7 +236,7 @@
         for k, (a, c) in enumerate(chunks[:direct]):
             def one(pt, pj, p):
                 copy(part(p, a, c), recv.at[members + me, :, pl.ds(a, c)],
-                     send_b, recv_b.at[k], mate, (pt, pj)).start()
+                     send_b, recv_a.at[k], mate, (pt, pj)).start()
             to_plane(one, True)
         for k in order[direct:]:
             push(k)
@@ -250,9 +244,9 @@
             a, c = chunks[k]
             if i == min(RAW_SENT, last - direct):
                 send_raw(beyond, members + me)
-            arrived(k)
+            settle(recv.at[pl.ds(0, members), :, pl.ds(a, c)], recv_a.at[k])
             copy(recv.at[pl.ds(0, members), :, pl.ds(a, c)], recv.at[pl.ds(members, members), :, pl.ds(a, c)],
-                 send_b, recv_b.at[k], mate, (t, j)).start()
+                 send_b, recv_a.at[k], mate, (t, j)).start()
         settle(far.at[pl.ds(0, members)], send_r)
         settle(recv.at[pl.ds(0, members)], send_b)
         settle(recv.at[pl.ds(0, members - 1), :, pl.ds(chunks[direct][0], mine - chunks[direct][0])], send_a)
@@ -283,7 +277,7 @@
                 vmem((2 * members, rows, mine)),
                 vmem((2 * members, rows, e)),
                 sems, sems((2,)),
-                sems, per_chunk, sems, per_chunk, sems, per_swap, sems, sems,
+                sems, per_chunk, sems, sems, per_swap, sems, sems,
                 sems, sems,
             ],
             compiler_params=pltpu.CompilerParams(

time: 38.7 us -> 38.4 us (level)
  Pallas kernels: 37.7 us -> 37.3 us
where the time goes in v4:
time: 38.4 us; the launch traced here: 38.2 us
  Pallas kernels  37.3 us (97%)
  local copies, waits for them, and re-layouts  0.88 us (2%)
    pallas_call x1, Pallas kernels, shards(): pl.pallas_call(functools.partial(kernel, nt, ns), out_shape=jax.ShapeDtyp...  37.3 us
    unnamed x1, local copies, waits for them, and re-layouts  0.88 us

profile of v4, /device:TPU:0, one launch (start us, length us, event | category | flops | bytes accessed | tf_op | source)
XLA Modules:
  0.0 38.2 jit_solution(11800493760278714553)
XLA Ops:
  0.0 37.3 %anomaly.1 = f32[4,49152]{1,0:T(4,128)S(1)} custom-call(f32[4,49152]{1,0:T(4,128)} %x_hbm.1, s32[1,128]{1,0:T(1,128)} %bitcast.2, s32[1,128]{1,0:T(1,128)} %bitcast.3), custom_call_target="tpu_custom_call" | custom-call | tf_op jit(solution)/shard_map/anomaly/pallas_call | solution.py:266
  37.3 0.9 %copy.5 = f32[4,49152]{1,0:T(4,128)} copy(f32[4,49152]{1,0:T(4,128)S(1)} %anomaly.1) | data formatting | bytes 1572864

commit v5 on v4

--- a/solution.py
+++ b/solution.py
@@ -9,10 +9,11 @@
 
 GROUPS = 46
 BASE_YEARS = 6
+PAIR = 2
 PLANES = 4
 UNIT = 128
 RAW = 8
-SIZES = (2, 3, 3, 4, 4, 4, 4, 4, 4, 3, 2, 1)
+SIZES = (2, 3, 3, 3, 3, 3, 3, 3, 3, 3, 3, 3, 2, 1)
 PIECES = 4
 DIRECT = 2
 LAG = 3
@@ -151,7 +152,7 @@
 
         bucket, season = calendar[0], calendar[1]
         key = jnp.where(season < BASE_YEARS, bucket, -1)
-        padded = sums.shape[0]
+        padded = GROUPS
         here = 2 * members * rows
 
         def half(first, second):
@@ -182,7 +183,7 @@
 
         def swap(k):
             a, c = chunks[k]
-            return copy(sums.at[:, pl.ds(a, c)], other.at[:, pl.ds(a, c)], send_s, recv_s.at[k], across, (t, j))
+            return copy(sums.at[:, :, pl.ds(a, c)], other.at[:, :, pl.ds(a, c)], send_s, recv_s.at[k], across, (t, j))
 
         def back(k, both):
             a, c = chunks[k]
@@ -202,7 +203,8 @@
         def finish(k):
             a, c = chunks[k]
             swap(k).wait_recv()
-            back(k, sums[:, pl.ds(a, c)] + other[:, pl.ds(a, c)])
+            both = sums[:, :, pl.ds(a, c)] + other[:, :, pl.ds(a, c)]
+            back(k, both.reshape(GROUPS, c))
 
         def finish_raw(k):
             a, c = chunks[k]
@@ -216,7 +218,7 @@
                 finish_raw(k)
                 continue
             a, c = chunks[k]
-            sums[:, pl.ds(a, c)] = total(k)
+            sums[:, :, pl.ds(a, c)] = total(k).reshape(GROUPS // PAIR, PAIR, c)
             swap(k).start()
             if k >= LAG:
                 finish(k - LAG)
@@ -272,8 +274,8 @@
                 pltpu.VMEM((2, 1, days), jnp.int32),
                 vmem((rows, cells)),
                 vmem((2 * members, rows, mine)),
-                vmem((GROUPS, mine - e)),
-                vmem((GROUPS, mine - e)),
+                vmem((GROUPS // PAIR, PAIR, mine - e)),
+                vmem((GROUPS // PAIR, PAIR, mine - e)),
                 vmem((2 * members, rows, mine)),
                 vmem((2 * members, rows, e)),
                 sems, sems((2,)),

time: 38.4 us -> 37.5 us (0.977)
  Pallas kernels: 37.3 us -> 36.4 us
    pallas_call x1, Pallas kernels: 37.3 us -> 36.4 us  [shards(): pl.pallas_call(functools.partial(kernel, nt, ns), out_shape=jax.ShapeDtyp...]
where the time goes in v5:
time: 37.5 us; the launch traced here: 37.3 us
  Pallas kernels  36.4 us (97%)
  local copies, waits for them, and re-layouts  0.88 us (2%)
    pallas_call x1, Pallas kernels, shards(): pl.pallas_call(functools.partial(kernel, nt, ns), out_shape=jax.ShapeDtyp...  36.4 us
    unnamed x1, local copies, waits for them, and re-layouts  0.88 us

profile of v5, /device:TPU:0, one launch (start us, length us, event | category | flops | bytes accessed | tf_op | source)
XLA Modules:
  0.0 37.3 jit_solution(18437776205560743053)
XLA Ops:
  0.0 36.4 %anomaly.1 = f32[4,49152]{1,0:T(4,128)S(1)} custom-call(f32[4,49152]{1,0:T(4,128)} %x_hbm.1, s32[1,128]{1,0:T(1,128)} %bitcast.2, s32[1,128]{1,0:T(1,128)} %bitcast.3), custom_call_target="tpu_custom_call" | custom-call | tf_op jit(solution)/shard_map/anomaly/pallas_call | solution.py:268
  36.4 0.9 %copy.5 = f32[4,49152]{1,0:T(4,128)} copy(f32[4,49152]{1,0:T(4,128)S(1)} %anomaly.1) | data formatting | bytes 1572864

commit v6 on v5

--- a/solution.py
+++ b/solution.py
@@ -50,13 +50,14 @@
     return members, units * UNIT, raw * UNIT, swapped, cuts((units - raw) * UNIT, raw, (1,) * PIECES)
 
 
-def kernel(nt, ns, x_hbm, bucket_hbm, season_hbm, out_ref, calendar, xv, recv, sums, other, y, far,
+def kernel(nt, ns, x_hbm, bucket_hbm, season_hbm, out_ref, calendar, xv, recv, y, far,
            load_sem, date_sem, send_a, recv_a, send_b, send_s, recv_s, send_o, recv_o,
-           send_r, recv_r):
+           send_r, recv_r, *pairs):
     rows, cells = x_hbm.shape
     w = ns // PLANES
     members, mine, e, swapped, raws = plan(nt, ns, cells)
     chunks = swapped + raws
+    sums, other = pairs[:len(swapped)], pairs[len(swapped):]
     last = len(swapped) - 1
     order = []
     for k in range(len(swapped)):
@@ -143,8 +144,8 @@
             date.start()
         pl.semaphore_wait(barrier, 2 * members - 1)
         load.wait()
+        send_raw(across, me)
         push(0)
-        send_raw(across, me)
         for k in order[1:]:
             push(k)
         for date in dates:
@@ -182,8 +183,7 @@
             return exact_dot(of_ours, recv[:, :, pl.ds(a, c)].reshape(here, c))
 
         def swap(k):
-            a, c = chunks[k]
-            return copy(sums.at[:, :, pl.ds(a, c)], other.at[:, :, pl.ds(a, c)], send_s, recv_s.at[k], across, (t, j))
+            return copy(sums[k], other[k], send_s, recv_s.at[k], across, (t, j))
 
         def back(k, both):
             a, c = chunks[k]
@@ -201,10 +201,8 @@
             out_ref[:, at] = y[me, :, cols]
 
         def finish(k):
-            a, c = chunks[k]
             swap(k).wait_recv()
-            both = sums[:, :, pl.ds(a, c)] + other[:, :, pl.ds(a, c)]
-            back(k, both.reshape(GROUPS, c))
+            back(k, (sums[k][...] + other[k][...]).reshape(GROUPS, chunks[k][1]))
 
         def finish_raw(k):
             a, c = chunks[k]
@@ -217,15 +215,15 @@
             if k > last:
                 finish_raw(k)
                 continue
-            a, c = chunks[k]
-            sums[:, :, pl.ds(a, c)] = total(k).reshape(GROUPS // PAIR, PAIR, c)
+            sums[k][...] = total(k).reshape(sums[k].shape)
             swap(k).start()
             if k >= LAG:
                 finish(k - LAG)
         for k in range(max(len(swapped) - LAG, 0), len(swapped)):
             finish(k)
 
-        settle(sums, send_s)
+        for part_sums in sums:
+            settle(part_sums, send_s)
         settle(far.at[pl.ds(0, members)], send_r)
         settle(y.at[pl.ds(0, 2 * members - 1)], send_o)
         settle(recv.at[pl.ds(0, members - 1)], recv_o)
@@ -274,13 +272,12 @@
                 pltpu.VMEM((2, 1, days), jnp.int32),
                 vmem((rows, cells)),
                 vmem((2 * members, rows, mine)),
-                vmem((GROUPS // PAIR, PAIR, mine - e)),
-                vmem((GROUPS // PAIR, PAIR, mine - e)),
                 vmem((2 * members, rows, mine)),
                 vmem((2 * members, rows, e)),
                 sems, sems((2,)),
                 sems, per_chunk, sems, sems, per_swap, sems, sems,
                 sems, sems,
+                *[vmem((GROUPS // PAIR, PAIR, c)) for _, c in swapped * 2],
             ],
             compiler_params=pltpu.CompilerParams(
                 collective_id=0, has_side_effects=True, vmem_limit_bytes=30 * 2**20),

time: 37.5 us -> 37.5 us (level)
  no operation moved by 1% of the time
where the time goes in v6:
time: 37.5 us; the launch traced here: 37.3 us
  Pallas kernels  36.4 us (97%)
  local copies, waits for them, and re-layouts  0.88 us (2%)
    pallas_call x1, Pallas kernels, shards(): pl.pallas_call(functools.partial(kernel, nt, ns), out_shape=jax.ShapeDtyp...  36.4 us
    unnamed x1, local copies, waits for them, and re-layouts  0.88 us

profile of v6, /device:TPU:0, one launch (start us, length us, event | category | flops | bytes accessed | tf_op | source)
XLA Modules:
  0.0 37.3 jit_solution(786017311175350544)
XLA Ops:
  0.0 36.4 %anomaly.1 = f32[4,49152]{1,0:T(4,128)S(1)} custom-call(f32[4,49152]{1,0:T(4,128)} %x_hbm.1, s32[1,128]{1,0:T(1,128)} %bitcast.2, s32[1,128]{1,0:T(1,128)} %bitcast.3), custom_call_target="tpu_custom_call" | custom-call | tf_op jit(solution)/shard_map/anomaly/pallas_call | solution.py:266
  36.4 0.9 %copy.5 = f32[4,49152]{1,0:T(4,128)} copy(f32[4,49152]{1,0:T(4,128)S(1)} %anomaly.1) | data formatting | bytes 1572864
